TPU v7x, 32 devices: a whole 2x2x4 slice. The times are simulated.
32 devices in a mesh: grid: 4 (over y, x), fsdp: 8 (over z, core).
Axes of the slice: x: 2, y: 2, z: 4, core: 2. Of those that a mesh axis runs over, the one named last changes fastest.
Arguments:
- hidden: bfloat16 [512, 4096], P('fsdp'), may hold values from -16 to 16
- norm_gain: float32 [4096], replicated, may hold values from 0.5 to 1.5
- base_head: bfloat16 [8192, 4096], P('fsdp'), may hold values from -1 to 1
- first_dir: bfloat16 [8192, 4096], P('fsdp'), may hold values from -0.09375 to 0.09375
- second_dir: bfloat16 [8192, 4096], P('fsdp'), may hold values from -0.09375 to 0.09375
- coords: int32 [8, 2], P('grid'), parts along dimension 0, may hold values from 0 to 7
- targets: int32 [512], replicated, may hold values from 0 to 8191
Outputs:
- token_loss: float32 [8, 512], P('grid', 'fsdp'), parts along dimension 0
- mean_loss: float32 [8], P('grid'), parts along dimension 0
There are 4 independent parts, one for each index of `grid`. A program takes and returns all parts, laid end to end along the dimension named above; an argument that names none is the same for every part. Nothing has to cross between parts.
All inputs are finite; a program needn't handle non-finite values.
Results may differ from a plain program's by a relative error of at most 0.0003.
Values may be sent and summed in bfloat16 or wider, within the bound.
A program may use at most 128 MiB of HBM per device.

v0:
```python
import functools

import jax
import jax.numpy as jnp
from jax import lax
from jax.experimental import pallas as pl
from jax.experimental.pallas import tpu as pltpu
from jax.sharding import PartitionSpec as P

epsilon = 1e-05
MESH = pl.DeviceIdType.MESH
NUM_PIECES = 16
ROW_CHUNK = 64


def kernel(
    n_grid, n_fsdp, total_tokens,
    coords_ref, hidden_hbm, gain_ref, targets_ref, base_ref, first_ref, second_ref,
    packed_ref,
    hidden_ref, hidden_sem, w_buf, x_buf, acc, mix_own, mix_all, stat_own, stat_all,
    w_sem, up_sem, dn_sem, pt_sem, recv_sem, recv_pt_sem,
    mix_send, mix_recv, stat_send, stat_recv, known_sem,
):
    g = lax.axis_index("grid")
    f = lax.axis_index("fsdp")
    n_chips = n_fsdp // 2
    z, core = f // 2, f % 2
    n_all = n_grid * n_fsdp
    me = g * n_fsdp + f
    pts = coords_ref.shape[0]
    own, width = hidden_hbm.shape
    vocab = base_ref.shape[0]
    kp = x_buf.shape[2]
    lanes = x_buf.shape[1]
    is_root = z == g
    go_up = jnp.logical_and(z >= g, z < n_chips - 1)
    go_dn = jnp.logical_and(z <= g, z > 0)

    def w_copy(j, p):
        src = (base_ref, first_ref, second_ref)[j]
        cols = pl.ds(pl.multiple_of(p * kp, kp), kp)
        return pltpu.make_async_copy(src.at[:, cols], w_buf.at[j, p], w_sem.at[j, p])

    barrier = pltpu.get_barrier_semaphore()
    for d in range(1, n_fsdp):
        pl.semaphore_signal(
            barrier, inc=1, device_id=(g, lax.rem(f + d, n_fsdp)), device_id_type=MESH
        )
    for d in range(1, n_grid):
        pl.semaphore_signal(
            barrier, inc=1, device_id=(lax.rem(g + d, n_grid), f), device_id_type=MESH
        )

    @pl.when(is_root)
    def _():
        pltpu.make_async_copy(hidden_hbm, hidden_ref, hidden_sem).start()


    for pt in range(pts):
        for k in range(2):
            level = jnp.full((1, lanes), coords_ref[pt, k], jnp.int32).astype(jnp.float32)
            mix_own[2 * pt + k : 2 * pt + k + 1, :] = (2.0 * level - 7.0) / 7.0
    mix_all[pl.ds(g, 1)] = mix_own[...][None]

    mine = pl.ds(pl.multiple_of(core * own, own), own)

    @pl.when(is_root)
    def _():
        pltpu.make_async_copy(hidden_hbm, hidden_ref, hidden_sem).wait()
        squares = jnp.zeros((own, 1), jnp.float32)
        for p in range(NUM_PIECES):
            wide = hidden_ref[:, p * kp : (p + 1) * kp].astype(jnp.float32)
            squares = squares + jnp.sum(wide * wide, axis=1, keepdims=True)
        inv_rms = lax.rsqrt(squares / width + epsilon)
        for p in range(NUM_PIECES):
            wide = hidden_ref[:, p * kp : (p + 1) * kp].astype(jnp.float32)
            gain = gain_ref[:, p * kp : (p + 1) * kp]
            x_buf[p, mine, :] = (wide * inv_rms * gain).astype(jnp.bfloat16)

    pl.semaphore_wait(barrier, n_fsdp + n_grid - 2)

    def x_copy(p, send_sem, sem, target):
        return pltpu.make_async_remote_copy(
            src_ref=x_buf.at[p, mine], dst_ref=x_buf.at[p, mine],
            send_sem=send_sem.at[p], recv_sem=sem.at[p],
            device_id=(g, target), device_id_type=MESH,
        )

    partner = f + 1 - 2 * core
    above = lax.rem(f + 2, n_fsdp)
    below = lax.rem(f + n_fsdp - 2, n_fsdp)

    def send_on(p):
        @pl.when(go_up)
        def _():
            x_copy(p, up_sem, recv_sem, above).start()

        @pl.when(go_dn)
        def _():
            x_copy(p, dn_sem, recv_sem, below).start()

        x_copy(p, pt_sem, recv_pt_sem, partner).start()

    @pl.when(is_root)
    def _():
        @pl.loop(0, NUM_PIECES)
        def _(p):
            send_on(p)

    def mix_copy(d):
        to = lax.rem(g + d, n_grid)
        return pltpu.make_async_remote_copy(
            src_ref=mix_own, dst_ref=mix_all.at[g],
            send_sem=mix_send.at[d - 1], recv_sem=mix_recv.at[g],
            device_id=(to, f), device_id_type=MESH,
        )

    for d in range(1, n_grid):
        pl.semaphore_signal(
            known_sem, inc=1, device_id=(lax.rem(g + d, n_grid), f), device_id_type=MESH
        )
        mix_copy(d).start()

    @pl.loop(0, NUM_PIECES)
    def _(p):
        for j in range(3):
            w_copy(j, p).start()

    acc[...] = jnp.zeros_like(acc)

    def compute(p):
        other = pl.ds(pl.multiple_of((1 - core) * own, own), own)
        pltpu.make_async_remote_copy(
            src_ref=x_buf.at[p, other], dst_ref=x_buf.at[p, other],
            send_sem=pt_sem.at[p], recv_sem=recv_pt_sem.at[p],
            device_id=(g, partner), device_id_type=MESH,
        ).wait_recv()
        for j in range(3):
            w_copy(j, p).wait()
        for j in range(3):
            acc[j] += lax.dot_general(
                w_buf[j, p], x_buf[p], (((1,), (1,)), ((), ())),
                preferred_element_type=jnp.float32,
            )

    @pl.loop(0, NUM_PIECES)
    def _(p):
        @pl.when(jnp.logical_not(is_root))
        def _():
            x_copy(p, up_sem, recv_sem, above).wait_recv()
            send_on(p)

        @pl.when(p > 0)
        def _():
            compute(p - 1)

    compute(NUM_PIECES - 1)

    for d in range(1, n_grid):
        pltpu.make_async_remote_copy(
            src_ref=mix_own, dst_ref=mix_all.at[lax.rem(g + d, n_grid)],
            send_sem=mix_send.at[d - 1], recv_sem=mix_recv.at[lax.rem(g + d, n_grid)],
            device_id=(lax.rem(g + d, n_grid), f), device_id_type=MESH,
        ).wait_recv()

    n_pts = n_grid * pts
    coef = []
    for pt in range(n_pts):
        rows = [mix_all[pt // pts, 2 * (pt % pts) + k : 2 * (pt % pts) + k + 1, :] for k in range(2)]
        coef.append([jnp.broadcast_to(r, (8, lanes)) for r in rows])

    targets = targets_ref[pl.ds(g, 1), :] - f * vocab
    steps = vocab // ROW_CHUNK
    tall = ROW_CHUNK // 8

    def block(c):
        rows = pl.ds(pl.multiple_of(c * ROW_CHUNK, ROW_CHUNK), ROW_CHUNK)
        return [acc[j, rows, :].reshape(tall, 8, lanes) for j in range(3)]

    def mixed(parts, pt):
        return parts[0] + coef[pt][0][None] * parts[1] + coef[pt][1][None] * parts[2]

    sub = lax.broadcasted_iota(jnp.int32, (tall, 8, lanes), 0) * 8 + lax.broadcasted_iota(
        jnp.int32, (tall, 8, lanes), 1
    )

    def top_step(c, carry):
        tops, picks = carry
        parts = block(c)
        hit = sub == (targets - c * ROW_CHUNK)[None]
        picks = tuple(
            pk + jnp.sum(jnp.where(hit, part, 0.0), axis=0) for pk, part in zip(picks, parts)
        )
        tops = tuple(
            jnp.maximum(tops[pt], jnp.max(mixed(parts, pt), axis=0)) for pt in range(n_pts)
        )
        return tops, picks

    low = jnp.full((8, lanes), -jnp.inf, jnp.float32)
    zero = jnp.zeros((8, lanes), jnp.float32)
    tops, picks = lax.fori_loop(0, steps, top_step, ((low,) * n_pts, (zero,) * 3))
    tops = [jnp.broadcast_to(jnp.max(t, axis=0, keepdims=True), (8, lanes)) for t in tops]
    picks = [jnp.sum(pk, axis=0, keepdims=True) for pk in picks]

    def sum_step(c, sums):
        parts = block(c)
        return tuple(
            sums[pt] + jnp.sum(jnp.exp(mixed(parts, pt) - tops[pt][None]), axis=0)
            for pt in range(n_pts)
        )

    sums = lax.fori_loop(0, steps, sum_step, (zero,) * n_pts)
    for pt in range(n_pts):
        at, row = pt // pts, pt % pts
        total = jnp.sum(sums[pt], axis=0, keepdims=True)
        stat_own[at, row : row + 1, :] = tops[pt][0:1] + jnp.log(total)
        stat_own[at, pts + row : pts + row + 1, :] = (
            picks[0] + coef[pt][0][0:1] * picks[1] + coef[pt][1][0:1] * picks[2]
        )
    stat_all[pl.ds(f, 1), pl.ds(g, 1)] = stat_own[pl.ds(g, 1)][None]

    @pl.loop(0, NUM_PIECES)
    def _(p):
        @pl.when(go_up)
        def _():
            x_copy(p, up_sem, recv_sem, above).wait_send()

        @pl.when(go_dn)
        def _():
            x_copy(p, dn_sem, recv_sem, below).wait_send()

        x_copy(p, pt_sem, recv_pt_sem, partner).wait_send()

    for d in range(1, n_grid):
        mix_copy(d).wait_send()
    pl.semaphore_wait(known_sem, n_grid - 1)

    def stat_copy(d):
        to = lax.rem(me + d, n_all)
        return pltpu.make_async_remote_copy(
            src_ref=stat_own.at[to // n_fsdp], dst_ref=stat_all.at[f, g],
            send_sem=stat_send.at[d - 1], recv_sem=stat_recv.at[me],
            device_id=(to // n_fsdp, lax.rem(to, n_fsdp)), device_id_type=MESH,
        )

    @pl.loop(1, n_all)
    def _(d):
        stat_copy(d).start()

    @pl.loop(1, n_all)
    def _(d):
        frm = lax.rem(me + d, n_all)
        fg, ff = frm // n_fsdp, lax.rem(frm, n_fsdp)
        pltpu.make_async_remote_copy(
            src_ref=stat_own.at[0], dst_ref=stat_all.at[ff, fg],
            send_sem=stat_send.at[d - 1], recv_sem=stat_recv.at[frm],
            device_id=(fg, ff), device_id_type=MESH,
        ).wait_recv()

    everything = jnp.zeros((pts, lanes), jnp.float32)
    chosen = jnp.zeros((pts, lanes), jnp.float32)
    for column in range(n_grid):
        here = stat_all[:, column]
        lse = here[:, :pts]
        top = jnp.max(lse, axis=0)
        loss = top + jnp.log(jnp.sum(jnp.exp(lse - top[None]), axis=0))
        loss = loss - jnp.sum(here[:, pts:], axis=0)
        everything = everything + loss
        chosen = jnp.where(z == column, loss, chosen)
    packed_ref[:pts, :own] = jnp.where(core == 0, chosen[:, :own], chosen[:, own:])
    for pt in range(pts):
        mean = jnp.sum(everything[pt : pt + 1, :], axis=1, keepdims=True) / total_tokens
        packed_ref[pts + pt : pts + pt + 1, :] = jnp.broadcast_to(mean, (1, lanes))

    @pl.loop(1, n_all)
    def _(d):
        stat_copy(d).wait_send()


def split(packed_ref, token_ref, mean_ref):
    pts, own = token_ref.shape
    token_ref[...] = packed_ref[:pts, :own]
    for pt in range(pts):
        mean_ref[pt] = packed_ref[pts + pt, 0]


def body(n_grid, n_fsdp, hidden, norm_gain, base_head, first_dir, second_dir, coords, targets):
    own, width = hidden.shape
    vocab = base_head.shape[0]
    pts = coords.shape[0]
    total = targets.shape[0]
    lanes = total // n_grid
    assert lanes == 2 * own and n_fsdp == 2 * n_grid
    kp = width // NUM_PIECES
    n_all = n_grid * n_fsdp
    dma = pltpu.SemaphoreType.DMA
    vmem = pl.BlockSpec(memory_space=pltpu.VMEM)
    smem = pl.BlockSpec(memory_space=pltpu.SMEM)
    anywhere = pl.BlockSpec(memory_space=pl.ANY)
    packed = pl.pallas_call(
        functools.partial(kernel, n_grid, n_fsdp, total),
        out_shape=jax.ShapeDtypeStruct((2 * pts, lanes), jnp.float32),
        in_specs=[smem, anywhere, vmem, vmem, anywhere, anywhere, anywhere],
        out_specs=vmem,
        scratch_shapes=[
            pltpu.VMEM((own, width), jnp.bfloat16),
            dma,
            pltpu.VMEM((3, NUM_PIECES, vocab, kp), jnp.bfloat16),
            pltpu.VMEM((NUM_PIECES, lanes, kp), jnp.bfloat16),
            pltpu.VMEM((3, vocab, lanes), jnp.float32),
            pltpu.VMEM((2 * pts, lanes), jnp.float32),
            pltpu.VMEM((n_grid, 2 * pts, lanes), jnp.float32),
            pltpu.VMEM((n_grid, 2 * pts, lanes), jnp.float32),
            pltpu.VMEM((n_fsdp, n_grid, 2 * pts, lanes), jnp.float32),
            dma((3, NUM_PIECES)),
            dma((NUM_PIECES,)),
            dma((NUM_PIECES,)),
            dma((NUM_PIECES,)),
            dma((NUM_PIECES,)),
            dma((NUM_PIECES,)),
            dma((n_grid - 1,)),
            dma((n_grid,)),
            dma((n_all - 1,)),
            dma((n_all,)),
            pltpu.SemaphoreType.REGULAR,
        ],
        compiler_params=pltpu.CompilerParams(
            collective_id=0, has_side_effects=True, vmem_limit_bytes=60 * 1024 * 1024
        ),
    )(
        coords, hidden, norm_gain.reshape(1, width), targets.reshape(n_grid, lanes),
        base_head, first_dir, second_dir,
    )
    return tuple(
        pl.pallas_call(
            split,
            out_shape=(
                jax.ShapeDtypeStruct((pts, own), jnp.float32),
                jax.ShapeDtypeStruct((pts,), jnp.float32),
            ),
            in_specs=[vmem],
            out_specs=(vmem, smem),
        )(packed)
    )


def solution(mesh):
    placed = (
        P("fsdp", None),
        P(),
        P("fsdp", None),
        P("fsdp", None),
        P("fsdp", None),
        P("grid", None),
        P(),
    )
    n_grid, n_fsdp = mesh.shape["grid"], mesh.shape["fsdp"]
    return jax.shard_map(
        functools.partial(body, n_grid, n_fsdp),
        mesh=mesh, in_specs=placed, out_specs=(P("grid", "fsdp"), P("grid")), check_vma=False,
    )
```

profile of v0, /device:TPU:0, one launch (start us, length us, event | category | flops | bytes accessed | tf_op | source)
XLA Modules:
  0.0 40.1 jit_solution(11822176299209932188)
XLA Ops:
  0.6 38.2 %shard_map.86.packed_ref = f32[4,128]{1,0:T(4,128)} custom-call(s32[2,2]{1,0:T(2,128)} %coords_ref.1, bf16[64,4096]{1,0:T(8,128)(2,1)} %hidden_hbm.1, f32[1,4096]{1,0:T(1,128)} %bitcast.2, s32[4,128]{1,0:T(4,128)} %bitcast.3, bf16[1024,4096]{1,0:T(8,128)(2,1)} %base_ref.1, bf16[1024,4096]{1,0:T(8,128)(2,1)} %first_ref.1, bf16[1024,4096]{1,0:T(8,128)(2,1)} %second_ref.1), custom_call_target="tpu_custom_call" | custom-call | tf_op jit(solution)/shard_map/pallas_call | solution.py:300
  38.9 1.3 %shard_map.87 = (f32[2,64]{1,0:T(2,128)}, f32[2]{0:T(128)}) custom-call(f32[4,128]{1,0:T(4,128)} %shard_map.86.packed_ref), custom_call_target="tpu_custom_call" | custom-call | tf_op jit(solution)/shard_map/pallas_call | solution.py:335
where the time goes:
time: 40.4 us; the launch traced here: 40.1 us
  Pallas kernels  39.5 us (98%)
  between operations  0.64 us (2%)
    pallas_call x1, Pallas kernels, body(): pl.pallas_call(functools.partial(kernel, n_grid, n_fsdp, total), out_shap...  38.2 us
    pallas_call x1, Pallas kernels, body(): pl.pallas_call(split, out_shape=(jax.ShapeDtypeStruct((pts, own), jnp.flo...  1.26 us

commit v1 on v0

v1 whole, which is shorter than its diff:
```python
import functools

import jax
import jax.numpy as jnp
from jax import lax
from jax.experimental import pallas as pl
from jax.experimental.pallas import tpu as pltpu
from jax.sharding import PartitionSpec as P

epsilon = 1e-05
MESH = pl.DeviceIdType.MESH
NUM_PIECES = 8
ROW_CHUNK = 32
LOG2E = 1.4426950408889634
LN2 = 0.6931471805599453


def kernel(
    n_grid, n_fsdp, total_tokens,
    coords_hbm, hidden_hbm, gain_hbm, targets_hbm, base_hbm, first_hbm, second_hbm,
    packed_ref,
    coords_ref, hidden_ref, gain_ref, targets_ref,
    w_buf, x_buf, acc, mix_own, mix_all, stat_own, stat_all,
    small_sem, w_sem, chain_send, chain_recv, pair_send, pair_recv,
    mix_send, mix_recv, stat_send, stat_recv, known_sem,
):
    g = lax.axis_index("grid")
    f = lax.axis_index("fsdp")
    nz = n_fsdp // 2
    z, core = f // 2, f % 2
    n_all = n_grid * n_fsdp
    me = g * n_fsdp + f
    pts = coords_hbm.shape[0]
    chunk, width = hidden_ref.shape
    vocab = base_hbm.shape[0]
    kp = x_buf.shape[4]
    lanes = 2 * nz * chunk
    last = nz - 1
    is_end = jnp.logical_or(z == 0, z == last)

    barrier = pltpu.get_barrier_semaphore()
    for d in range(1, n_fsdp):
        pl.semaphore_signal(
            barrier, inc=1, device_id=(g, lax.rem(f + d, n_fsdp)), device_id_type=MESH
        )
    for d in range(1, n_grid):
        pl.semaphore_signal(
            barrier, inc=1, device_id=(lax.rem(g + d, n_grid), f), device_id_type=MESH
        )

    rows = pl.ds(pl.multiple_of(g * chunk, chunk), chunk)
    small = [
        pltpu.make_async_copy(hidden_hbm.at[rows, :], hidden_ref, small_sem.at[0]),
        pltpu.make_async_copy(gain_hbm, gain_ref, small_sem.at[1]),
        pltpu.make_async_copy(coords_hbm, coords_ref, small_sem.at[2]),
        pltpu.make_async_copy(targets_hbm, targets_ref, small_sem.at[3]),
    ]
    for copy in small:
        copy.start()

    @pl.loop(0, NUM_PIECES)
    def _(p):
        cols = pl.ds(pl.multiple_of(p * kp, kp), kp)
        for j, src in enumerate((base_hbm, first_hbm, second_hbm)):
            pltpu.make_async_copy(src.at[:, cols], w_buf.at[p, j], w_sem.at[p]).start()

    small[0].wait()
    small[1].wait()
    squares = jnp.zeros((chunk, 1), jnp.float32)
    for p in range(NUM_PIECES):
        wide = hidden_ref[:, p * kp : (p + 1) * kp].astype(jnp.float32)
        squares = squares + jnp.sum(wide * wide, axis=1, keepdims=True)
    inv_rms = lax.rsqrt(squares / width + epsilon)
    for p in range(NUM_PIECES):
        wide = hidden_ref[:, p * kp : (p + 1) * kp].astype(jnp.float32)
        gain = gain_ref[:, p * kp : (p + 1) * kp]
        x_buf[p, pl.ds(core, 1), pl.ds(z, 1)] = (
            (wide * inv_rms * gain).astype(jnp.bfloat16)[None, None]
        )

    pl.semaphore_wait(barrier, n_fsdp + n_grid - 2)

    def chain_copy(p, s, target):
        return pltpu.make_async_remote_copy(
            src_ref=x_buf.at[p, core, s], dst_ref=x_buf.at[p, core, s],
            send_sem=chain_send, recv_sem=chain_recv.at[p, s],
            device_id=(g, 2 * target + core), device_id_type=MESH,
        )

    def pair_copy(p, s):
        return pltpu.make_async_remote_copy(
            src_ref=x_buf.at[p, core, s], dst_ref=x_buf.at[p, core, s],
            send_sem=pair_send, recv_sem=pair_recv.at[p],
            device_id=(g, f + 1 - 2 * core), device_id_type=MESH,
        )

    @pl.loop(0, NUM_PIECES)
    def _(p):
        @pl.when(is_end)
        def _():
            for i in range(last):
                chain_copy(p, z, jnp.where(z == 0, last - i, i)).start()

        @pl.when(jnp.logical_not(is_end))
        def _():
            chain_copy(p, z, z + 1).start()
            chain_copy(p, z, z - 1).start()

        pair_copy(p, z).start()

    small[2].wait()
    for pt in range(pts):
        for k in range(2):
            level = jnp.broadcast_to(coords_ref[pt : pt + 1, k : k + 1], (1, lanes))
            mix_own[2 * pt + k : 2 * pt + k + 1, :] = (2.0 * level.astype(jnp.float32) - 7.0) / 7.0
    mix_all[pl.ds(g, 1)] = mix_own[...][None]

    def mix_copy(d):
        return pltpu.make_async_remote_copy(
            src_ref=mix_own, dst_ref=mix_all.at[g],
            send_sem=mix_send, recv_sem=mix_recv,
            device_id=(lax.rem(g + d, n_grid), f), device_id_type=MESH,
        )

    for d in range(1, n_grid):
        pl.semaphore_signal(
            known_sem, inc=1, device_id=(lax.rem(g + d, n_grid), f), device_id_type=MESH
        )
        mix_copy(d).start()

    acc[...] = jnp.zeros_like(acc)

    sign = jnp.where(2 * z < nz, 1, -1)

    def take_in(p):
        for d in range(1, nz):
            s = lax.rem(z + nz + sign * d, nz)
            chain_copy(p, s, z).wait_recv()

            @pl.when(jnp.logical_and(jnp.logical_and(s < z, s > 0), z < last))
            def _():
                chain_copy(p, s, z + 1).start()

            @pl.when(jnp.logical_and(jnp.logical_and(s > z, s < last), z > 0))
            def _():
                chain_copy(p, s, z - 1).start()

            pair_copy(p, s).start()

    def compute(p):
        pltpu.make_async_remote_copy(
            src_ref=x_buf.at[p, 1 - core], dst_ref=x_buf.at[p, 1 - core],
            send_sem=pair_send, recv_sem=pair_recv.at[p],
            device_id=(g, f + 1 - 2 * core), device_id_type=MESH,
        ).wait_recv()
        pltpu.make_async_copy(w_buf.at[p], w_buf.at[p], w_sem.at[p]).wait()
        x = x_buf[p].reshape(lanes, kp)
        for j in range(3):
            acc[j] += lax.dot_general(
                w_buf[p, j], x, (((1,), (1,)), ((), ())),
                preferred_element_type=jnp.float32,
            )

    @pl.loop(0, NUM_PIECES)
    def _(p):
        take_in(p)

        @pl.when(p > 0)
        def _():
            compute(p - 1)

    compute(NUM_PIECES - 1)

    pltpu.make_async_copy(
        mix_all.at[: n_grid - 1], mix_all.at[: n_grid - 1], mix_recv
    ).wait()
    small[3].wait()

    n_pts = n_grid * pts
    coef = []
    for pt in range(n_pts):
        r = 2 * (pt % pts)
        coef.append([mix_all[pt // pts, r + k : r + k + 1, :] for k in range(2)])
    scaled = [[jnp.broadcast_to(LOG2E * v, (8, lanes)) for v in pair] for pair in coef]

    lane_chunk = lax.rem(lax.broadcasted_iota(jnp.int32, (8, lanes), 1) // chunk, nz)
    targets = jnp.zeros((8, lanes), jnp.int32)
    for s in range(nz):
        row = jnp.broadcast_to(targets_ref[s : s + 1, :], (8, lanes))
        row = pltpu.roll(row, lax.rem((s - g) * chunk + lanes, lanes), 1)
        targets = jnp.where(lane_chunk == s, row, targets)
    targets = targets - f * vocab

    tall = ROW_CHUNK // 8
    sub = lax.broadcasted_iota(jnp.int32, (tall, 8, lanes), 0) * 8 + lax.broadcasted_iota(
        jnp.int32, (tall, 8, lanes), 1
    )

    def step(c, carry):
        tops, sums, picks = carry
        at = pl.ds(pl.multiple_of(c * ROW_CHUNK, ROW_CHUNK), ROW_CHUNK)
        parts = [acc[j, at, :].reshape(tall, 8, lanes) for j in range(3)]
        hit = sub == (targets - c * ROW_CHUNK)[None]
        picks = tuple(
            pk + jnp.sum(jnp.where(hit, part, 0.0), axis=0) for pk, part in zip(picks, parts)
        )
        centre = LOG2E * parts[0]
        new_tops, new_sums = [], []
        for pt in range(n_pts):
            logit = centre + scaled[pt][0][None] * parts[1] + scaled[pt][1][None] * parts[2]
            top = jnp.maximum(tops[pt], jnp.max(logit, axis=0))
            new_sums.append(
                sums[pt] * jnp.exp2(tops[pt] - top)
                + jnp.sum(jnp.exp2(logit - top[None]), axis=0)
            )
            new_tops.append(top)
        return tuple(new_tops), tuple(new_sums), picks

    low = jnp.full((8, lanes), -jnp.inf, jnp.float32)
    zero = jnp.zeros((8, lanes), jnp.float32)
    tops, sums, picks = lax.fori_loop(
        0, vocab // ROW_CHUNK, step, ((low,) * n_pts, (zero,) * n_pts, (zero,) * 3)
    )
    picks = [jnp.sum(pk, axis=0, keepdims=True) for pk in picks]
    for pt in range(n_pts):
        at, row = pt // pts, pt % pts
        top = jnp.max(tops[pt], axis=0, keepdims=True)
        total = jnp.sum(sums[pt] * jnp.exp2(tops[pt] - top), axis=0, keepdims=True)
        stat_own[at, row : row + 1, :] = LN2 * top + jnp.log(total)
        stat_own[at, pts + row : pts + row + 1, :] = (
            picks[0] + coef[pt][0] * picks[1] + coef[pt][1] * picks[2]
        )
    stat_all[pl.ds(me, 1)] = stat_own[pl.ds(g, 1)]

    pltpu.make_async_copy(
        x_buf.at[:, 0, :last], x_buf.at[:, 0, :last], chain_send
    ).wait()
    pltpu.make_async_copy(x_buf.at[:, 0], x_buf.at[:, 0], pair_send).wait()
    pltpu.make_async_copy(
        mix_all.at[: n_grid - 1], mix_all.at[: n_grid - 1], mix_send
    ).wait()
    pl.semaphore_wait(known_sem, n_grid - 1)

    @pl.loop(1, n_all)
    def _(d):
        to = lax.rem(me + d, n_all)
        tg, tf = to // n_fsdp, lax.rem(to, n_fsdp)
        pltpu.make_async_remote_copy(
            src_ref=stat_own.at[tg], dst_ref=stat_all.at[me],
            send_sem=stat_send, recv_sem=stat_recv,
            device_id=(tg, tf), device_id_type=MESH,
        ).start()

    others = stat_all.at[: n_all - 1]
    pltpu.make_async_copy(others, others, stat_recv).wait()

    everything = jnp.zeros((pts, lanes), jnp.float32)
    chosen = jnp.zeros((pts, lanes), jnp.float32)
    lane = lax.broadcasted_iota(jnp.int32, (pts, lanes), 1)
    start = core * nz * chunk + z * chunk
    for column in range(n_grid):
        here = stat_all[column * n_fsdp : (column + 1) * n_fsdp]
        lse = here[:, :pts]
        top = jnp.max(lse, axis=0)
        loss = top + jnp.log(jnp.sum(jnp.exp(lse - top[None]), axis=0))
        loss = loss - jnp.sum(here[:, pts:], axis=0)
        everything = everything + loss
        moved = pltpu.roll(loss, lax.rem(column * chunk + lanes - start, lanes), 1)
        chosen = jnp.where(lane // chunk == column, moved, chosen)
    packed_ref[:pts, :] = chosen
    for pt in range(pts):
        mean = jnp.sum(everything[pt : pt + 1, :], axis=1, keepdims=True) / total_tokens
        packed_ref[pts + pt : pts + pt + 1, :] = jnp.broadcast_to(mean, (1, lanes))

    pltpu.make_async_copy(others, others, stat_send).wait()


def split(packed_ref, token_ref, mean_ref):
    pts, own = token_ref.shape
    token_ref[...] = packed_ref[:pts, :own]
    for pt in range(pts):
        mean_ref[pt] = packed_ref[pts + pt, 0]


def body(n_grid, n_fsdp, hidden, norm_gain, base_head, first_dir, second_dir, coords, targets):
    own, width = hidden.shape
    vocab = base_head.shape[0]
    pts = coords.shape[0]
    total = targets.shape[0]
    nz = n_fsdp // 2
    chunk = own // n_grid
    lanes = 2 * nz * chunk
    assert nz == n_grid and own == nz * chunk and total == n_grid * lanes
    kp = width // NUM_PIECES
    n_all = n_grid * n_fsdp
    dma = pltpu.SemaphoreType.DMA
    vmem = pl.BlockSpec(memory_space=pltpu.VMEM)
    smem = pl.BlockSpec(memory_space=pltpu.SMEM)
    anywhere = pl.BlockSpec(memory_space=pl.ANY)
    packed = pl.pallas_call(
        functools.partial(kernel, n_grid, n_fsdp, total),
        out_shape=jax.ShapeDtypeStruct((2 * pts, lanes), jnp.float32),
        in_specs=[anywhere] * 7,
        out_specs=vmem,
        scratch_shapes=[
            pltpu.VMEM((pts, 2), jnp.int32),
            pltpu.VMEM((chunk, width), jnp.bfloat16),
            pltpu.VMEM((1, width), jnp.float32),
            pltpu.VMEM((nz, 2 * own), jnp.int32),
            pltpu.VMEM((NUM_PIECES, 3, vocab, kp), jnp.bfloat16),
            pltpu.VMEM((NUM_PIECES, 2, nz, chunk, kp), jnp.bfloat16),
            pltpu.VMEM((3, vocab, lanes), jnp.float32),
            pltpu.VMEM((2 * pts, lanes), jnp.float32),
            pltpu.VMEM((n_grid, 2 * pts, lanes), jnp.float32),
            pltpu.VMEM((n_grid, 2 * pts, lanes), jnp.float32),
            pltpu.VMEM((n_all, 2 * pts, lanes), jnp.float32),
            dma((4,)),
            dma((NUM_PIECES,)),
            dma,
            dma((NUM_PIECES, nz)),
            dma,
            dma((NUM_PIECES,)),
            dma,
            dma,
            dma,
            dma,
            pltpu.SemaphoreType.REGULAR,
        ],
        compiler_params=pltpu.CompilerParams(
            collective_id=0, has_side_effects=True, vmem_limit_bytes=60 * 1024 * 1024
        ),
    )(
        coords, hidden, norm_gain.reshape(1, width), targets.reshape(nz, 2 * own),
        base_head, first_dir, second_dir,
    )
    return tuple(
        pl.pallas_call(
            split,
            out_shape=(
                jax.ShapeDtypeStruct((pts, own), jnp.float32),
                jax.ShapeDtypeStruct((pts,), jnp.float32),
            ),
            in_specs=[vmem],
            out_specs=(vmem, smem),
        )(packed)
    )


def solution(mesh):
    placed = (
        P("fsdp", None),
        P(),
        P("fsdp", None),
        P("fsdp", None),
        P("fsdp", None),
        P("grid", None),
        P(),
    )
    n_grid, n_fsdp = mesh.shape["grid"], mesh.shape["fsdp"]
    return jax.shard_map(
        functools.partial(body, n_grid, n_fsdp),
        mesh=mesh, in_specs=placed, out_specs=(P("grid", "fsdp"), P("grid")), check_vma=False,
    )
```

time: 40.4 us -> 31.8 us (0.79)
  Pallas kernels: 39.5 us -> 31 us
    pallas_call x1, Pallas kernels: 38.2 us -> 29.8 us  [body(): pl.pallas_call(functools.partial(kernel, n_grid, n_fsdp, total), out_shap...]
where the time goes in v1:
time: 31.8 us; the launch traced here: 31.7 us
  Pallas kernels  31 us (97%)
  between operations  0.64 us (2%)
    pallas_call x1, Pallas kernels, body(): pl.pallas_call(functools.partial(kernel, n_grid, n_fsdp, total), out_shap...  29.8 us
    pallas_call x1, Pallas kernels, body(): pl.pallas_call(split, out_shape=(jax.ShapeDtypeStruct((pts, own), jnp.flo...  1.26 us

profile of v1, /device:TPU:0, one launch (start us, length us, event | category | flops | bytes accessed | tf_op | source)
XLA Modules:
  0.0 31.7 jit_solution(17455436325017450520)
XLA Ops:
  0.6 29.8 %shard_map.86.packed_ref = f32[4,128]{1,0:T(4,128)} custom-call(s32[2,2]{1,0:T(2,128)} %coords_hbm.1, bf16[64,4096]{1,0:T(8,128)(2,1)} %hidden_hbm.1, f32[1,4096]{1,0:T(1,128)} %bitcast.2, s32[4,128]{1,0:T(4,128)} %bitcast.3, bf16[1024,4096]{1,0:T(8,128)(2,1)} %base_hbm.1, bf16[1024,4096]{1,0:T(8,128)(2,1)} %first_hbm.1, bf16[1024,4096]{1,0:T(8,128)(2,1)} %second_hbm.1), custom_call_target="tpu_custom_call" | custom-call | tf_op jit(solution)/shard_map/pallas_call | solution.py:300
  30.4 1.3 %shard_map.87 = (f32[2,64]{1,0:T(2,128)}, f32[2]{0:T(128)}) custom-call(f32[4,128]{1,0:T(4,128)} %shard_map.86.packed_ref), custom_call_target="tpu_custom_call" | custom-call | tf_op jit(solution)/shard_map/pallas_call | solution.py:337
